TPU v7x, 128 devices: a whole 4x4x4 slice. The times are simulated.
128 devices in a mesh: head: 16 (over z, y), batch: 8 (over x, core).
Axes of the slice: x: 4, y: 4, z: 4, core: 2. Of those that a mesh axis runs over, the one named last changes fastest.
Arguments:
- incoming_hidden_stream: bfloat16 [1024, 4096], P('batch'), may hold values from -6 to 6
- reception_projection: bfloat16 [4096, 4096], P(None, 'head'), may hold values from -0.09375 to 0.09375
- address_projection: bfloat16 [4096, 4096], P(None, 'head'), may hold values from -0.09375 to 0.09375
- payload_projection: bfloat16 [4096, 4096], P(None, 'head'), may hold values from -0.09375 to 0.09375
- sigmoid_filter_matrix: bfloat16 [4096, 4096], P(None, 'head'), may hold values from -0.09375 to 0.09375
- forgetting_speed: float32 [1024, 4096], P('batch', 'head'), may hold values from 0.01 to 1.5
- adaptation_step_size: float32 [1024, 4096], P('batch', 'head'), may hold values from 0 to 1
- diagonal_boost: float32 [4096], P('head'), may hold values from -0.6 to 0.6
- subspace_standardize_scale: float32 [4096], P('head'), may hold values from 0.5 to 2
- recurrent_memory_matrix: float32 [128, 64, 64, 64], P('batch', 'head'), may hold values from -6 to 6
- emission_projection: bfloat16 [4096, 4096], P('head'), may hold values from -0.09375 to 0.09375
- closing_standardize_scale: float32 [4096], replicated, may hold values from 0.7 to 2
- lexicon_projection: bfloat16 [4096, 65536], P(None, ('head', 'batch')), may hold values from -32 to 32
- proposed_tokens_list: int32 [128, 8], P('batch'), may hold values from 0 to 65535
- threshold_milli_nats: int32 [128, 8], P('batch'), may hold values from -22000 to -10001
Outputs:
- new_state: float32 [128, 64, 64, 64], P('batch', 'head')
- margin: float32 [128, 8], P('batch')
- accept: float32 [128, 8], P('batch')
All inputs are finite; a program needn't handle non-finite values.
Results may differ from a plain program's by a relative error of at most 0.0017.
Values may be sent and summed in bfloat16 or wider, within the bound.
A program may use at most 128 MiB of HBM per device.

v0:
```python
import math
import jax
import jax.numpy as jnp
from jax import lax
from jax.sharding import Mesh
from jax.sharding import PartitionSpec as P

HEAD = ("head_0", "head_1")
HEAD_BATCH = ("head_0", "head_1", "batch")


def in_blocks(x, dim, size):
    before, after = (x.shape[:dim], x.shape[dim + 1 :])
    return jnp.moveaxis(x.reshape(*before, size, -1, *after), dim, 0)


def sent_and_summed(x, axis, dim):
    size = lax.axis_size(axis)
    parts = lax.all_to_all(in_blocks(x, dim, size), axis, 0, 0, tiled=True)
    return jnp.sum(parts, axis=0)


def by_axis(x, axes):
    for axis in axes:
        x = lax.psum(x, axis)
    return x


def joined_along(parts, dim):
    parts = jnp.moveaxis(parts, 0, dim)
    shape = parts.shape
    return parts.reshape(*shape[:dim], shape[dim] * shape[dim + 1], *shape[dim + 2 :])


def sent_to_all(x, axis):
    copies = jnp.broadcast_to(x, (lax.axis_size(axis), *x.shape))
    return lax.all_to_all(copies, axis, split_axis=0, concat_axis=0, tiled=True)


def gathered_copies(x, axis, dim):
    return joined_along(sent_to_all(x, axis), dim)


def gathered_once(x, axis):
    leaves = jax.tree.leaves(x)
    sequence = sorted(range(len(leaves)), key=lambda k: -leaves[k].size)
    width = (1, *leaves[sequence[0]].shape)[-1]
    lines = [
        jnp.pad(leaves[k].reshape(-1), (0, -leaves[k].size % width)).reshape(-1, width)
        for k in sequence
    ]
    both, at, found = (sent_to_all(jnp.concatenate(lines), axis), 0, {})
    for k, line in zip(sequence, lines):
        share = both[:, at : at + len(line)].reshape(len(both), -1)
        found[k] = share[:, : leaves[k].size].reshape(-1, *leaves[k].shape)
        at += len(line)
    numbers = iter(range(len(leaves)))
    return jax.tree.map(lambda _: found[next(numbers)], x)


def combined_pairwise(pieces, combine):
    while len(jax.tree.leaves(pieces)[0]) > 1:
        pieces = jax.vmap(combine)(
            *(jax.tree.map(lambda part: part[side::2], pieces) for side in (0, 1))
        )
    return jax.tree.map(lambda part: part[0], pieces)


def combined_all(x, axis, combine):
    pieces = gathered_once(x, axis)
    return combined_pairwise(pieces, combine)


def gathered_by_type(x, axis):
    leaves, found = (jax.tree.leaves(x), {})
    for initial, a in enumerate(leaves):
        if initial not in found:
            alike = [k for k, b in enumerate(leaves) if b.dtype == a.dtype]
            got = (
                gathered_once([leaves[k] for k in alike], axis)
                if len(alike) > 1
                else [sent_to_all(a, axis)]
            )
            for k, b in zip(alike, got):
                found[k] = b
    numbers = iter(range(len(leaves)))
    return jax.tree.map(lambda _: found[next(numbers)], x)


def merged(x, axis, combine):
    pieces = gathered_by_type(x, axis)
    return combined_pairwise(pieces, combine)


def advance(start, reception_vectors, address_vectors, payload_vectors, decay, rate):
    unit = (
        address_vectors
        * lax.rsqrt(jnp.mean(address_vectors * address_vectors, -1, keepdims=True) + 1e-06)
        / math.sqrt(address_vectors.shape[-1])
    )
    inputs = tuple(
        (
            jnp.moveaxis(item, 1, 0)
            for item in (reception_vectors, address_vectors, payload_vectors, decay, unit, rate)
        )
    )

    def step(current, pieces):
        recept_now, keys_now, values_now, decay_now, unit_now, rate_now = pieces
        recall = jnp.einsum("bhij,bhj->bhi", current, unit_now, precision=lax.Precision.HIGHEST)
        current = (
            current * decay_now[:, :, None, :]
            - recall[:, :, :, None] * (unit_now * rate_now)[:, :, None, :]
            + values_now[:, :, :, None] * keys_now[:, :, None, :]
        )
        output = jnp.einsum("bhij,bhj->bhi", current, recept_now, precision=lax.Precision.HIGHEST)
        return (current, output)

    final, outputs = lax.scan(step, start, inputs)
    return (final, jnp.moveaxis(outputs, 0, 1))


def combine_stats(first, second):
    top = jnp.maximum(first[0], second[0])
    summed = first[1] * jnp.exp(first[0] - top) + second[1] * jnp.exp(second[0] - top)
    return (top, summed, first[2] + second[2])


def local_stats(logits, ids_flat, offset):
    peak = jnp.max(logits, -1)
    total = jnp.sum(jnp.exp(logits - peak[:, None]), -1)
    column = lax.broadcasted_iota(jnp.int32, logits.shape, 1)
    target = jnp.sum(jnp.where(column == (ids_flat - offset)[:, None], logits, 0.0), -1)
    return (peak, total, target)


def shards(
    incoming_hidden_stream,
    reception_projection,
    address_projection,
    payload_projection,
    sigmoid_filter_matrix,
    forgetting_speed,
    adaptation_step_size,
    diagonal_boost,
    subspace_standardize_scale,
    recurrent_memory_matrix,
    emission_projection,
    closing_standardize_scale,
    lexicon_projection,
    proposed_tokens_list,
    threshold_milli_nats,
):
    seq_dev, draft_len = proposed_tokens_list.shape
    lanes_on_shard, subspace_size = (
        recurrent_memory_matrix.shape[1],
        recurrent_memory_matrix.shape[2],
    )
    tok_dev = seq_dev * draft_len
    width = incoming_hidden_stream.shape[1]
    shape4 = (seq_dev, draft_len, lanes_on_shard, subspace_size)
    reception_vectors = jnp.dot(
        incoming_hidden_stream, reception_projection, preferred_element_type=jnp.float32
    ).reshape(shape4)
    address_vectors = jnp.dot(
        incoming_hidden_stream, address_projection, preferred_element_type=jnp.float32
    ).reshape(shape4)
    payload_vectors = jnp.dot(
        incoming_hidden_stream, payload_projection, preferred_element_type=jnp.float32
    ).reshape(shape4)
    gate = jnp.dot(
        incoming_hidden_stream, sigmoid_filter_matrix, preferred_element_type=jnp.float32
    )
    decay = jnp.exp(-forgetting_speed).reshape(shape4)
    rate = adaptation_step_size.reshape(shape4)
    new_state, wkv = advance(
        recurrent_memory_matrix, reception_vectors, address_vectors, payload_vectors, decay, rate
    )
    center = wkv - jnp.mean(wkv, -1, keepdims=True)
    interpolated_embedding = (
        center
        * lax.rsqrt(jnp.mean(center * center, -1, keepdims=True) + 1e-05)
        * subspace_standardize_scale.reshape(lanes_on_shard, subspace_size)
    )
    interpolated_embedding = (
        interpolated_embedding
        + jnp.sum(
            reception_vectors
            * address_vectors
            * diagonal_boost.reshape(lanes_on_shard, subspace_size),
            -1,
            keepdims=True,
        )
        * payload_vectors
    )
    gated = (
        interpolated_embedding.reshape(tok_dev, lanes_on_shard * subspace_size)
        * jax.nn.sigmoid(gate)
    ).astype(jnp.bfloat16)
    partial_out = jnp.dot(gated, emission_projection, preferred_element_type=jnp.float32)
    share = sent_and_summed(partial_out, HEAD, 1)
    cols = share.shape[1]
    begin = lax.axis_index(HEAD) * cols
    residual = (
        lax.dynamic_slice_in_dim(incoming_hidden_stream, begin, cols, 1).astype(jnp.float32) + share
    )
    moment_one, moment_two = (
        by_axis(jnp.sum(residual, -1), HEAD),
        by_axis(jnp.sum(residual * residual, -1), HEAD),
    )
    mean_row = moment_one / width
    variance = moment_two / width - mean_row * mean_row
    gain_part = lax.dynamic_slice_in_dim(closing_standardize_scale, begin, cols, 0)
    normed_part = (
        (residual - mean_row[:, None]) * lax.rsqrt(variance + 1e-05)[:, None] * gain_part
    ).astype(jnp.bfloat16)
    normed = gathered_copies(normed_part, HEAD, 1)
    every, every_ids = (
        lax.all_gather(normed, "batch", axis=0, tiled=True),
        lax.all_gather(proposed_tokens_list, "batch", axis=0, tiled=True),
    )
    logits = jnp.dot(every, lexicon_projection, preferred_element_type=jnp.float32)
    vcols = lexicon_projection.shape[1]
    offset = (lax.axis_index(HEAD) * lax.axis_size("batch") + lax.axis_index("batch")) * vcols
    peak, total, target = local_stats(logits, every_ids.reshape(-1), offset)
    peak, total, target = combined_all((peak, total, target), "batch", combine_stats)
    row_begin = lax.axis_index("batch") * tok_dev
    peak = lax.dynamic_slice_in_dim(peak, row_begin, tok_dev, 0)
    total = lax.dynamic_slice_in_dim(total, row_begin, tok_dev, 0)
    target = lax.dynamic_slice_in_dim(target, row_begin, tok_dev, 0)
    top, summed, target = merged((peak, total, target), HEAD, combine_stats)
    logprob = target - (top + jnp.log(summed))
    margin = logprob.reshape(seq_dev, draft_len) - threshold_milli_nats.astype(jnp.float32) / 1000.0
    accept = jnp.cumprod(jax.nn.sigmoid(margin * 0.5), axis=1)
    return (new_state, margin, accept)


def solution(mesh):
    split = Mesh(mesh.devices.reshape(4, 4, mesh.shape["batch"]), ("head_0", "head_1", "batch"))
    return jax.shard_map(
        shards,
        mesh=split,
        in_specs=(
            P("batch", None),
            P(None, HEAD),
            P(None, HEAD),
            P(None, HEAD),
            P(None, HEAD),
            P("batch", HEAD),
            P("batch", HEAD),
            P(HEAD),
            P(HEAD),
            P("batch", HEAD, None, None),
            P(HEAD, None),
            P(),
            P(None, HEAD_BATCH),
            P("batch", None),
            P("batch", None),
        ),
        out_specs=(P("batch", HEAD, None, None), P("batch", None), P("batch", None)),
        check_vma=False,
    )
```

profile of v0, /device:TPU:0, one launch (start us, length us, event | category | flops | bytes accessed | tf_op | source)
XLA Modules:
  0.0 318.9 jit_solution(11417522193714851282)
XLA Ops:
  29.0 105.4 %while.12 = (s32[]{:T(128)}, f32[16,4,64,64]{3,2,1,0:T(8,128)}, f32[8,16,4,64]{3,2,1,0:T(4,128)S(1)}, f32[8,16,4,64]{3,2,0,1:T(4,128)}, f32[8,16,4,64]{3,2,1,0:T...) while((s32[]{:T(128)}, f32[16,4,64,64]{3,2,1,0:T(8,128)}, ...), condition=%wide.region_2.3_spmd, body=%wide.region_1.2_spmd.sunk | while | flops 7606274 | bytes 13009081 | solution.py:119
  31.5 4.9 %fusion.54 = f32[16,4,1,64]{3,2,1,0:T(1,128)S(1)} fusion(f32[16,4,64,1]{2,3,1,0:T(1,128)S(1)} %bitcast.118, f32[16,4,64,64]{3,2,1,0:T(8,128)} %get-tuple-element.245), kind=kOutput, calls=%fused_computation.79.clone.1 | convolution fusion | flops 3145728 | bytes 1081344 | tf_op jit(solution)/shard_map/while/body/eval_jaxpr/bhij,bhj->bhi/dot_general | solution.py:110
  44.7 4.9 %fusion.54 = f32[16,4,1,64]{3,2,1,0:T(1,128)S(1)} fusion(f32[16,4,64,1]{2,3,1,0:T(1,128)S(1)} %bitcast.118, f32[16,4,64,64]{3,2,1,0:T(8,128)} %get-tuple-element.245), kind=kOutput, calls=%fused_computation.79.clone.1 | convolution fusion | flops 3145728 | bytes 1081344 | tf_op jit(solution)/shard_map/while/body/eval_jaxpr/bhij,bhj->bhi/dot_general | solution.py:110
  52.0 3.3 %fusion.55 = f32[16,4,1,64]{3,2,1,0:T(1,128)S(1)} fusion(f32[16,4,64,64]{3,2,1,0:T(8,128)S(1)} %multiply_add_fusion.8, f32[16,4,64,1]{2,3,1,0:T(1,128)S(1)} %bitcast.117), kind=kOutput, calls=%fused_computation.80.clone.1 | convolution fusion | flops 3145728 | bytes 1081344 | tf_op jit(solution)/shard_map/while/body/eval_jaxpr/bhij,bhj->bhi/dot_general | solution.py:116
  57.9 4.9 %fusion.54 = f32[16,4,1,64]{3,2,1,0:T(1,128)S(1)} fusion(f32[16,4,64,1]{2,3,1,0:T(1,128)S(1)} %bitcast.118, f32[16,4,64,64]{3,2,1,0:T(8,128)} %get-tuple-element.245), kind=kOutput, calls=%fused_computation.79.clone.1 | convolution fusion | flops 3145728 | bytes 1081344 | tf_op jit(solution)/shard_map/while/body/eval_jaxpr/bhij,bhj->bhi/dot_general | solution.py:110
  71.0 4.9 %fusion.54 = f32[16,4,1,64]{3,2,1,0:T(1,128)S(1)} fusion(f32[16,4,64,1]{2,3,1,0:T(1,128)S(1)} %bitcast.118, f32[16,4,64,64]{3,2,1,0:T(8,128)} %get-tuple-element.245), kind=kOutput, calls=%fused_computation.79.clone.1 | convolution fusion | flops 3145728 | bytes 1081344 | tf_op jit(solution)/shard_map/while/body/eval_jaxpr/bhij,bhj->bhi/dot_general | solution.py:110
  78.3 3.3 %fusion.55 = f32[16,4,1,64]{3,2,1,0:T(1,128)S(1)} fusion(f32[16,4,64,64]{3,2,1,0:T(8,128)S(1)} %multiply_add_fusion.8, f32[16,4,64,1]{2,3,1,0:T(1,128)S(1)} %bitcast.117), kind=kOutput, calls=%fused_computation.80.clone.1 | convolution fusion | flops 3145728 | bytes 1081344 | tf_op jit(solution)/shard_map/while/body/eval_jaxpr/bhij,bhj->bhi/dot_general | solution.py:116
  84.2 4.9 %fusion.54 = f32[16,4,1,64]{3,2,1,0:T(1,128)S(1)} fusion(f32[16,4,64,1]{2,3,1,0:T(1,128)S(1)} %bitcast.118, f32[16,4,64,64]{3,2,1,0:T(8,128)} %get-tuple-element.245), kind=kOutput, calls=%fused_computation.79.clone.1 | convolution fusion | flops 3145728 | bytes 1081344 | tf_op jit(solution)/shard_map/while/body/eval_jaxpr/bhij,bhj->bhi/dot_general | solution.py:110
  97.4 4.9 %fusion.54 = f32[16,4,1,64]{3,2,1,0:T(1,128)S(1)} fusion(f32[16,4,64,1]{2,3,1,0:T(1,128)S(1)} %bitcast.118, f32[16,4,64,64]{3,2,1,0:T(8,128)} %get-tuple-element.245), kind=kOutput, calls=%fused_computation.79.clone.1 | convolution fusion | flops 3145728 | bytes 1081344 | tf_op jit(solution)/shard_map/while/body/eval_jaxpr/bhij,bhj->bhi/dot_general | solution.py:110
  110.6 4.9 %fusion.54 = f32[16,4,1,64]{3,2,1,0:T(1,128)S(1)} fusion(f32[16,4,64,1]{2,3,1,0:T(1,128)S(1)} %bitcast.118, f32[16,4,64,64]{3,2,1,0:T(8,128)} %get-tuple-element.245), kind=kOutput, calls=%fused_computation.79.clone.1 | convolution fusion | flops 3145728 | bytes 1081344 | tf_op jit(solution)/shard_map/while/body/eval_jaxpr/bhij,bhj->bhi/dot_general | solution.py:110
  123.8 4.9 %fusion.54 = f32[16,4,1,64]{3,2,1,0:T(1,128)S(1)} fusion(f32[16,4,64,1]{2,3,1,0:T(1,128)S(1)} %bitcast.118, f32[16,4,64,64]{3,2,1,0:T(8,128)} %get-tuple-element.245), kind=kOutput, calls=%fused_computation.79.clone.1 | convolution fusion | flops 3145728 | bytes 1081344 | tf_op jit(solution)/shard_map/while/body/eval_jaxpr/bhij,bhj->bhi/dot_general | solution.py:110
  139.9 4.2 %fusion.5 = f32[128,4096]{1,0:T(8,128)} fusion(bf16[256,4096]{1,0:T(8,128)(2,1)S(1)} %copy-done, f32[128,256]{1,0:T(8,128)S(1)} %reshape.129, bf16[128,4096]{1,0:T(8,128)(2,1)S(1)} %copy-done.3, bf16[4096,256]{1,0:T(8,128)(2,1)} %param.21), kind=kOutput, calls=%fused_computation.18 | convolution fusion | flops 537034752 | bytes 7471104 | tf_op jit(solution)/shard_map/dot_general | solution.py:200
  147.3 8.2 %all-to-all-start = ((f32[16,128,256]{2,1,0:T(8,128)}), f32[16,128,256]{2,1,0:T(8,128)}, u32[]{:S(2)}, u32[]{:S(2)}) async-start(f32[16,128,256]{2,1,0:T(8,128)} %bitcast.113), calls=%async_computation | async-start | bytes 4194304 | tf_op jit(solution)/shard_map/all_to_all | solution.py:19
  156.4 31.0 %all-to-all-done = f32[16,128,256]{2,1,0:T(8,128)} async-done(((f32[16,128,256]{2,1,0:T(8,128)}), f32[16,128,256]{2,1,0:T(8,128)}, u32[]{:S(2)}, u32[]{:S(2)}) %all-to-all-start) | async-done | bytes 2097184 | tf_op jit(solution)/shard_map/all_to_all | solution.py:19
  189.2 9.5 %all-reduce.1 = (f32[128]{0:T(128)S(1)}, f32[128]{0:T(128)S(1)}) all-reduce(f32[128]{0:T(128)S(1)} %get-tuple-element.107, f32[128]{0:T(128)S(1)} %get-tuple-element.106), channel_id=1, replica_groups=mesh['head_0'=4,'head_1'=4,'batch'=8] {'head_0'}, use_global_device_ids=true, to_apply=%region_11.12 | all-reduce | flops 256 | bytes 2048 | tf_op jit(solution)/shard_map/psum | solution.py:25
  198.7 7.7 %all-reduce = (f32[128]{0:T(128)S(1)}, f32[128]{0:T(128)S(1)}) all-reduce(f32[128]{0:T(128)S(1)} %get-tuple-element.130, f32[128]{0:T(128)S(1)} %get-tuple-element.131), channel_id=1, replica_groups=mesh['head_0'=4,'head_1'=4,'batch'=8] {'head_1'}, use_global_device_ids=true, to_apply=%region_12.13 | all-reduce | flops 256 | bytes 2048 | tf_op jit(solution)/shard_map/psum | solution.py:25
  206.9 16.6 %all_to_all.20 = bf16[16,128,256]{1,2,0:T(8,128)(2,1)} all-to-all(bf16[16,128,256]{1,2,0:T(8,128)(2,1)S(1)} %broadcast_in_dim.21), channel_id=1, replica_groups=mesh['head_0'=4,'head_1'=4,'batch'=8] {'head_0','head_1'}, dimensions={0} | all-to-all | bytes 2097152 | tf_op jit(solution)/shard_map/all_to_all | solution.py:37
  223.5 13.3 %all-gather = s32[8,16,8]{1,2,0:T(8,128)S(1)} all-gather(s32[1,16,8]{1,2,0:T(8,128)S(1)} %bitcast.136), channel_id=1, replica_groups=mesh['head_0'=4,'head_1'=4,'batch'=8] {'batch'}, dimensions={0}, use_global_device_ids=true | all-gather | bytes 4608 | tf_op jit(solution)/shard_map/all_gather | solution.py:220
  237.0 37.6 %all-gather.3.cloned.1.call-done = bf16[1024,4096]{0,1:T(8,128)(2,1)} async-done(((bf16[128,4096]{0,1:T(8,128)(2,1)}), bf16[1024,4096]{0,1:T(8,128)(2,1)}) %all-gather.3.cloned.1.call-update) | async-done | bytes 8388624 | tf_op jit(solution)/shard_map/all_gather | solution.py:219
  274.6 8.3 %fusion.23 = (f32[1024]{0:T(1024)S(1)}, f32[1024,512]{0,1:T(8,128)S(1)}) fusion(bf16[1024,4096]{0,1:T(8,128)(2,1)} %all-gather.3.cloned.1.call-done, bf16[4096,512]{1,0:T(8,128)(2,1)} %param.29), kind=kOutput, calls=%fused_computation.78 | convolution fusion | flops 4295490560 | bytes 14684160 | tf_op jit(solution)/shard_map/dot_general | solution.py:222
  284.1 4.0 %all-to-all-start.2 = ((f32[8,3,1024]{2,1,0:T(4,128)}), f32[8,3,1024]{2,1,0:T(4,128)S(1)}, u32[]{:S(2)}, u32[]{:S(2)}) async-start(f32[8,3,1024]{2,1,0:T(4,128)} %broadcast_in_dim.23), calls=%async_computation.2 | async-start | bytes 262144 | tf_op jit(solution)/shard_map/all_to_all | solution.py:37
  288.1 6.1 %all-to-all-done.2 = f32[8,3,1024]{2,1,0:T(4,128)S(1)} async-done(((f32[8,3,1024]{2,1,0:T(4,128)}), f32[8,3,1024]{2,1,0:T(4,128)S(1)}, u32[]{:S(2)}, u32[]{:S(2)}) %all-to-all-start.2) | async-done | bytes 98336 | tf_op jit(solution)/shard_map/all_to_all | solution.py:37
  295.4 6.9 %all-to-all-start.3 = ((f32[16,3,128]{2,1,0:T(4,128)}), f32[16,3,128]{2,1,0:T(4,128)S(1)}, u32[]{:S(2)}, u32[]{:S(2)}) async-start(f32[16,3,128]{2,1,0:T(4,128)} %broadcast_in_dim.25), calls=%async_computation.3 | async-start | bytes 65536 | tf_op jit(solution)/shard_map/all_to_all | solution.py:37
  302.5 7.5 %all-to-all-done.3 = f32[16,3,128]{2,1,0:T(4,128)S(1)} async-done(((f32[16,3,128]{2,1,0:T(4,128)}), f32[16,3,128]{2,1,0:T(4,128)S(1)}, u32[]{:S(2)}, u32[]{:S(2)}) %all-to-all-start.3) | async-done | bytes 24608 | tf_op jit(solution)/shard_map/all_to_all | solution.py:37
  (206 shorter events, 97.0 us)
Async XLA Ops:
  7.2 132.8 %copy-start = (bf16[256,4096]{1,0:T(8,128)(2,1)S(1)}, bf16[256,4096]{1,0:T(8,128)(2,1)}, u32[]{:S(2)}) copy-start(bf16[256,4096]{1,0:T(8,128)(2,1)} %param.27) | copy-start | bytes 6291460
  7.2 5.1 %copy-start.3 = (bf16[128,4096]{1,0:T(8,128)(2,1)S(1)}, bf16[128,4096]{1,0:T(8,128)(2,1)}, u32[]{:S(2)}) copy-start(bf16[128,4096]{1,0:T(8,128)(2,1)} %param.17) | copy-start | bytes 3145732
  14.3 3.7 %copy-start.7 = (f32[256]{0:T(256)S(1)}, f32[256]{0:T(256)}, u32[]{:S(2)}) copy-start(f32[256]{0:T(256)} %param.24) | copy-start | bytes 3076
  29.0 105.5 %copy-start.4 = (f32[16,8,4]{2,1,0:T(8,128)S(1)}, f32[16,8,4]{2,1,0:T(8,128)}, u32[]{:S(2)}) copy-start(f32[16,8,4]{2,1,0:T(8,128)} %get-tuple-element.108) | copy-start | bytes 6148
  29.0 106.1 %copy-start.8 = (f32[256]{0:T(256)S(1)}, f32[256]{0:T(256)}, u32[]{:S(2)}) copy-start(f32[256]{0:T(256)} %param.25) | copy-start | bytes 3076
  29.0 8.2 %copy-start.1 = (f32[16,4,64,64]{3,2,1,0:T(8,128)S(1)}, f32[16,4,64,64]{3,2,1,0:T(8,128)}, u32[]{:S(2)}) copy-start(f32[16,4,64,64]{3,2,1,0:T(8,128)} %get-tuple-element.245) | copy-start | bytes 3145732 | tf_op jit(solution)/shard_map/while
  38.8 3.4 %copy-start.2 = (f32[16,4,64,64]{3,2,1,0:T(8,128)}, f32[16,4,64,64]{3,2,1,0:T(8,128)S(1)}, u32[]{:S(2)}) copy-start(f32[16,4,64,64]{3,2,1,0:T(8,128)S(1)} %multiply_add_fusion.8) | copy-start | bytes 3145732 | tf_op jit(solution)/shard_map/while
  42.2 8.2 %copy-start.1 = (f32[16,4,64,64]{3,2,1,0:T(8,128)S(1)}, f32[16,4,64,64]{3,2,1,0:T(8,128)}, u32[]{:S(2)}) copy-start(f32[16,4,64,64]{3,2,1,0:T(8,128)} %get-tuple-element.245) | copy-start | bytes 3145732 | tf_op jit(solution)/shard_map/while
  51.9 3.4 %copy-start.2 = (f32[16,4,64,64]{3,2,1,0:T(8,128)}, f32[16,4,64,64]{3,2,1,0:T(8,128)S(1)}, u32[]{:S(2)}) copy-start(f32[16,4,64,64]{3,2,1,0:T(8,128)S(1)} %multiply_add_fusion.8) | copy-start | bytes 3145732 | tf_op jit(solution)/shard_map/while
  55.3 8.2 %copy-start.1 = (f32[16,4,64,64]{3,2,1,0:T(8,128)S(1)}, f32[16,4,64,64]{3,2,1,0:T(8,128)}, u32[]{:S(2)}) copy-start(f32[16,4,64,64]{3,2,1,0:T(8,128)} %get-tuple-element.245) | copy-start | bytes 3145732 | tf_op jit(solution)/shard_map/while
  68.5 8.2 %copy-start.1 = (f32[16,4,64,64]{3,2,1,0:T(8,128)S(1)}, f32[16,4,64,64]{3,2,1,0:T(8,128)}, u32[]{:S(2)}) copy-start(f32[16,4,64,64]{3,2,1,0:T(8,128)} %get-tuple-element.245) | copy-start | bytes 3145732 | tf_op jit(solution)/shard_map/while
  78.3 3.4 %copy-start.2 = (f32[16,4,64,64]{3,2,1,0:T(8,128)}, f32[16,4,64,64]{3,2,1,0:T(8,128)S(1)}, u32[]{:S(2)}) copy-start(f32[16,4,64,64]{3,2,1,0:T(8,128)S(1)} %multiply_add_fusion.8) | copy-start | bytes 3145732 | tf_op jit(solution)/shard_map/while
  81.7 8.2 %copy-start.1 = (f32[16,4,64,64]{3,2,1,0:T(8,128)S(1)}, f32[16,4,64,64]{3,2,1,0:T(8,128)}, u32[]{:S(2)}) copy-start(f32[16,4,64,64]{3,2,1,0:T(8,128)} %get-tuple-element.245) | copy-start | bytes 3145732 | tf_op jit(solution)/shard_map/while
  94.9 8.2 %copy-start.1 = (f32[16,4,64,64]{3,2,1,0:T(8,128)S(1)}, f32[16,4,64,64]{3,2,1,0:T(8,128)}, u32[]{:S(2)}) copy-start(f32[16,4,64,64]{3,2,1,0:T(8,128)} %get-tuple-element.245) | copy-start | bytes 3145732 | tf_op jit(solution)/shard_map/while
  104.7 3.4 %copy-start.2 = (f32[16,4,64,64]{3,2,1,0:T(8,128)}, f32[16,4,64,64]{3,2,1,0:T(8,128)S(1)}, u32[]{:S(2)}) copy-start(f32[16,4,64,64]{3,2,1,0:T(8,128)S(1)} %multiply_add_fusion.8) | copy-start | bytes 3145732 | tf_op jit(solution)/shard_map/while
  108.1 8.2 %copy-start.1 = (f32[16,4,64,64]{3,2,1,0:T(8,128)S(1)}, f32[16,4,64,64]{3,2,1,0:T(8,128)}, u32[]{:S(2)}) copy-start(f32[16,4,64,64]{3,2,1,0:T(8,128)} %get-tuple-element.245) | copy-start | bytes 3145732 | tf_op jit(solution)/shard_map/while
  121.3 8.2 %copy-start.1 = (f32[16,4,64,64]{3,2,1,0:T(8,128)S(1)}, f32[16,4,64,64]{3,2,1,0:T(8,128)}, u32[]{:S(2)}) copy-start(f32[16,4,64,64]{3,2,1,0:T(8,128)} %get-tuple-element.245) | copy-start | bytes 3145732 | tf_op jit(solution)/shard_map/while
  131.0 3.4 %copy-start.2 = (f32[16,4,64,64]{3,2,1,0:T(8,128)}, f32[16,4,64,64]{3,2,1,0:T(8,128)S(1)}, u32[]{:S(2)}) copy-start(f32[16,4,64,64]{3,2,1,0:T(8,128)S(1)} %multiply_add_fusion.8) | copy-start | bytes 3145732 | tf_op jit(solution)/shard_map/while
  147.3 40.1 %all-to-all-start = ((f32[16,128,256]{2,1,0:T(8,128)}), f32[16,128,256]{2,1,0:T(8,128)}, u32[]{:S(2)}, u32[]{:S(2)}) async-start(f32[16,128,256]{2,1,0:T(8,128)} %bitcast.113), calls=%async_computation | async-start | bytes 4194304 | tf_op jit(solution)/shard_map/all_to_all | solution.py:19
  155.5 119.1 %all-gather.3.cloned.1.call-start = ((), (), s32[]{:S(2)}) async-start(), calls=%async_computation.4 | async-start | bytes 9437184 | tf_op jit(solution)/shard_map/all_gather | solution.py:219
  206.7 16.9 %copy-start.5 = (s32[16,8]{0,1:T(8,128)S(1)}, s32[16,8]{0,1:T(8,128)}, u32[]{:S(2)}) copy-start(s32[16,8]{0,1:T(8,128)} %param.30) | copy-start | bytes 1540
  282.9 19.5 %copy-start.6 = (s32[16,8]{0,1:T(8,128)S(1)}, s32[16,8]{0,1:T(8,128)}, u32[]{:S(2)}) copy-start(s32[16,8]{0,1:T(8,128)} %param.31) | copy-start | bytes 1540
  284.1 10.1 %all-to-all-start.2 = ((f32[8,3,1024]{2,1,0:T(4,128)}), f32[8,3,1024]{2,1,0:T(4,128)S(1)}, u32[]{:S(2)}, u32[]{:S(2)}) async-start(f32[8,3,1024]{2,1,0:T(4,128)} %broadcast_in_dim.23), calls=%async_computation.2 | async-start | bytes 262144 | tf_op jit(solution)/shard_map/all_to_all | solution.py:37
  295.4 14.6 %all-to-all-start.3 = ((f32[16,3,128]{2,1,0:T(4,128)}), f32[16,3,128]{2,1,0:T(4,128)S(1)}, u32[]{:S(2)}, u32[]{:S(2)}) async-start(f32[16,3,128]{2,1,0:T(4,128)} %broadcast_in_dim.25), calls=%async_computation.3 | async-start | bytes 65536 | tf_op jit(solution)/shard_map/all_to_all | solution.py:37
  (3 other events, 10.1 us)
Sparse Core Ops, SparseCore 0:
  223.6 50.9 all-gather.2
where the time goes:
time: 321 us; the launch traced here: 319 us
  matrix products  84.9 us (26%)
  waiting for transfers between devices  82.3 us (26%)
  blocking collectives  47.1 us (15%)
  local copies, waits for them, and re-layouts  41.7 us (13%)
  other arithmetic  29.1 us (9%)
  starting transfers between devices  19.2 us (6%)
  between operations  14.4 us (4%)
    dot_general x8, matrix products, step(): jnp.einsum('bhij,bhj->bhi', current, unit_now, precision=lax.Precision.HI...  39.5 us
    all_gather x1, waiting for transfers between devices, shards(): lax.all_gather(normed, 'batch', axis=0, tiled=True)  37.6 us
    all_to_all x1, waiting for transfers between devices, sent_and_summed(): parts = lax.all_to_all(in_blocks(x, dim, size), axis, 0, 0, tiled=True)  31 us
    dot_general x8, matrix products, step(): jnp.einsum('bhij,bhj->bhi', current, recept_now, precision=lax.Precision....  26.8 us
    psum x2, blocking collectives, by_axis(): x = lax.psum(x, axis)  17.2 us
    all_to_all x1, blocking collectives, sent_to_all(): return lax.all_to_all(copies, axis, split_axis=0, concat_axis=0, tiled=True)  16.6 us
    all_to_all x2, waiting for transfers between devices, sent_to_all(): return lax.all_to_all(copies, axis, split_axis=0, concat_axis=0, tiled=True)  13.6 us
    all_gather x1, blocking collectives, shards(): lax.all_gather(proposed_tokens_list, 'batch', axis=0, tiled=True)  13.3 us
  transfers between devices with their start and end apart: 4, of which 4 were waited for; matrix products, arithmetic and copies ran while one was open for 0% of the time, Pallas kernels for 0%

commit v1 on v0

--- a/solution.py
+++ b/solution.py
@@ -216,7 +216,9 @@
     ).astype(jnp.bfloat16)
     normed = gathered_copies(normed_part, HEAD, 1)
     every, every_ids = (
-        lax.all_gather(normed, "batch", axis=0, tiled=True),
+        jnp.concatenate(
+            lax.all_to_all(jnp.stack([normed] * lax.axis_size("batch")), "batch", 0, 0), axis=0
+        ),
         lax.all_gather(proposed_tokens_list, "batch", axis=0, tiled=True),
     )
     logits = jnp.dot(every, lexicon_projection, preferred_element_type=jnp.float32)

time: 321 us -> 364 us (1.13)
  blocking collectives: 47.1 us -> 134 us
  waiting for transfers between devices: 82.3 us -> 44.6 us
  between operations: 14.4 us -> 1.05 us
  local copies, waits for them, and re-layouts: 41.7 us -> 47.4 us
    all_gather x1, blocking collectives: 13.3 us -> 100 us  [shards(): lax.all_gather(proposed_tokens_list, 'batch', axis=0, tiled=True)]
    all_gather x1 -> x0, waiting for transfers between devices: 37.6 us -> none  [shards(): lax.all_gather(normed, 'batch', axis=0, tiled=True)]
    another operation x0 -> x2, local copies, waits for them, and re-layouts: none -> 5.74 us  [shards(): jnp.stack([normed] * lax.axis_size('batch'))]
    all_to_all x0 -> x1, starting transfers between devices: none -> 5.09 us  [shards(): lax.all_to_all(jnp.stack([normed] * lax.axis_size('batch')), 'batch', 0, 0)]
    all_to_all x2, starting transfers between devices: 10.9 us -> 6.86 us  [sent_to_all(): return lax.all_to_all(copies, axis, split_axis=0, concat_axis=0, tiled=True)]
  transfers between devices with their start and end apart: 4 -> 4, of which waited for: 4 -> 3; matrix products, arithmetic and copies ran while one was open for 0% -> 0% of each run, Pallas kernels for 0% -> 0%
where the time goes in v1:
time: 364 us; the launch traced here: 362 us
  blocking collectives  134 us (37%)
  matrix products  84.9 us (23%)
  local copies, waits for them, and re-layouts  47.4 us (13%)
  waiting for transfers between devices  44.6 us (12%)
  other arithmetic  29.1 us (8%)
  starting transfers between devices  20.2 us (6%)
    all_gather x1, blocking collectives, shards(): lax.all_gather(proposed_tokens_list, 'batch', axis=0, tiled=True)  100 us
    dot_general x8, matrix products, step(): jnp.einsum('bhij,bhj->bhi', current, unit_now, precision=lax.Precision.HI...  39.5 us
    all_to_all x1, waiting for transfers between devices, sent_and_summed(): parts = lax.all_to_all(in_blocks(x, dim, size), axis, 0, 0, tiled=True)  31.1 us
    dot_general x8, matrix products, step(): jnp.einsum('bhij,bhj->bhi', current, recept_now, precision=lax.Precision....  26.8 us
    psum x2, blocking collectives, by_axis(): x = lax.psum(x, axis)  17.2 us
    all_to_all x1, blocking collectives, sent_to_all(): return lax.all_to_all(copies, axis, split_axis=0, concat_axis=0, tiled=True)  16.6 us
    all_to_all x2, waiting for transfers between devices, sent_to_all(): return lax.all_to_all(copies, axis, split_axis=0, concat_axis=0, tiled=True)  13.5 us
    add x8, other arithmetic, step(): current * decay_now[:, :, None, :]  12.3 us
  transfers between devices with their start and end apart: 4, of which 3 were waited for; matrix products, arithmetic and copies ran while one was open for 0% of the time, Pallas kernels for 0%

profile of v1, /device:TPU:0, one launch (start us, length us, event | category | flops | bytes accessed | tf_op | source)
XLA Modules:
  0.0 361.8 jit_solution(11618878034084453268)
XLA Ops:
  22.4 105.5 %while.12 = (s32[]{:T(128)}, f32[16,4,64,64]{3,2,1,0:T(8,128)}, f32[8,16,4,64]{3,2,1,0:T(4,128)S(1)}, f32[8,16,4,64]{3,2,0,1:T(4,128)}, f32[8,16,4,64]{3,2,1,0:T...) while((s32[]{:T(128)}, f32[16,4,64,64]{3,2,1,0:T(8,128)}, ...), condition=%wide.region_2.3_spmd, body=%wide.region_1.2_spmd.sunk | while | flops 7606274 | bytes 13009081 | solution.py:119
  25.0 4.9 %fusion.54 = f32[16,4,1,64]{3,2,1,0:T(1,128)S(1)} fusion(f32[16,4,64,1]{2,3,1,0:T(1,128)S(1)} %bitcast.119, f32[16,4,64,64]{3,2,1,0:T(8,128)} %get-tuple-element.245), kind=kOutput, calls=%fused_computation.79.clone.1 | convolution fusion | flops 3145728 | bytes 1081344 | tf_op jit(solution)/shard_map/while/body/eval_jaxpr/bhij,bhj->bhi/dot_general | solution.py:110
  38.1 4.9 %fusion.54 = f32[16,4,1,64]{3,2,1,0:T(1,128)S(1)} fusion(f32[16,4,64,1]{2,3,1,0:T(1,128)S(1)} %bitcast.119, f32[16,4,64,64]{3,2,1,0:T(8,128)} %get-tuple-element.245), kind=kOutput, calls=%fused_computation.79.clone.1 | convolution fusion | flops 3145728 | bytes 1081344 | tf_op jit(solution)/shard_map/while/body/eval_jaxpr/bhij,bhj->bhi/dot_general | solution.py:110
  51.3 4.9 %fusion.54 = f32[16,4,1,64]{3,2,1,0:T(1,128)S(1)} fusion(f32[16,4,64,1]{2,3,1,0:T(1,128)S(1)} %bitcast.119, f32[16,4,64,64]{3,2,1,0:T(8,128)} %get-tuple-element.245), kind=kOutput, calls=%fused_computation.79.clone.1 | convolution fusion | flops 3145728 | bytes 1081344 | tf_op jit(solution)/shard_map/while/body/eval_jaxpr/bhij,bhj->bhi/dot_general | solution.py:110
  64.5 4.9 %fusion.54 = f32[16,4,1,64]{3,2,1,0:T(1,128)S(1)} fusion(f32[16,4,64,1]{2,3,1,0:T(1,128)S(1)} %bitcast.119, f32[16,4,64,64]{3,2,1,0:T(8,128)} %get-tuple-element.245), kind=kOutput, calls=%fused_computation.79.clone.1 | convolution fusion | flops 3145728 | bytes 1081344 | tf_op jit(solution)/shard_map/while/body/eval_jaxpr/bhij,bhj->bhi/dot_general | solution.py:110
  71.8 3.3 fusion.55
  77.7 4.9 %fusion.54 = f32[16,4,1,64]{3,2,1,0:T(1,128)S(1)} fusion(f32[16,4,64,1]{2,3,1,0:T(1,128)S(1)} %bitcast.119, f32[16,4,64,64]{3,2,1,0:T(8,128)} %get-tuple-element.245), kind=kOutput, calls=%fused_computation.79.clone.1 | convolution fusion | flops 3145728 | bytes 1081344 | tf_op jit(solution)/shard_map/while/body/eval_jaxpr/bhij,bhj->bhi/dot_general | solution.py:110
  90.9 4.9 %fusion.54 = f32[16,4,1,64]{3,2,1,0:T(1,128)S(1)} fusion(f32[16,4,64,1]{2,3,1,0:T(1,128)S(1)} %bitcast.119, f32[16,4,64,64]{3,2,1,0:T(8,128)} %get-tuple-element.245), kind=kOutput, calls=%fused_computation.79.clone.1 | convolution fusion | flops 3145728 | bytes 1081344 | tf_op jit(solution)/shard_map/while/body/eval_jaxpr/bhij,bhj->bhi/dot_general | solution.py:110
  104.1 4.9 %fusion.54 = f32[16,4,1,64]{3,2,1,0:T(1,128)S(1)} fusion(f32[16,4,64,1]{2,3,1,0:T(1,128)S(1)} %bitcast.119, f32[16,4,64,64]{3,2,1,0:T(8,128)} %get-tuple-element.245), kind=kOutput, calls=%fused_computation.79.clone.1 | convolution fusion | flops 3145728 | bytes 1081344 | tf_op jit(solution)/shard_map/while/body/eval_jaxpr/bhij,bhj->bhi/dot_general | solution.py:110
  117.2 4.9 %fusion.54 = f32[16,4,1,64]{3,2,1,0:T(1,128)S(1)} fusion(f32[16,4,64,1]{2,3,1,0:T(1,128)S(1)} %bitcast.119, f32[16,4,64,64]{3,2,1,0:T(8,128)} %get-tuple-element.245), kind=kOutput, calls=%fused_computation.79.clone.1 | convolution fusion | flops 3145728 | bytes 1081344 | tf_op jit(solution)/shard_map/while/body/eval_jaxpr/bhij,bhj->bhi/dot_general | solution.py:110
  133.4 4.2 %fusion.5 = f32[128,4096]{1,0:T(8,128)} fusion(bf16[256,4096]{1,0:T(8,128)(2,1)S(1)} %copy-done, f32[128,256]{1,0:T(8,128)S(1)} %reshape.131, bf16[128,4096]{1,0:T(8,128)(2,1)S(1)} %copy-done.3, bf16[4096,256]{1,0:T(8,128)(2,1)} %param.21), kind=kOutput, calls=%fused_computation.18 | convolution fusion | flops 537034752 | bytes 7471104 | tf_op jit(solution)/shard_map/dot_general | solution.py:200
  140.8 8.2 %all-to-all-start = ((f32[16,128,256]{2,1,0:T(8,128)}), f32[16,128,256]{2,1,0:T(8,128)}, u32[]{:S(2)}, u32[]{:S(2)}) async-start(f32[16,128,256]{2,1,0:T(8,128)} %bitcast.114), calls=%async_computation | async-start | bytes 4194304 | tf_op jit(solution)/shard_map/all_to_all | solution.py:19
  149.8 31.1 %all-to-all-done = f32[16,128,256]{2,1,0:T(8,128)} async-done(((f32[16,128,256]{2,1,0:T(8,128)}), f32[16,128,256]{2,1,0:T(8,128)}, u32[]{:S(2)}, u32[]{:S(2)}) %all-to-all-start) | async-done | bytes 2097184 | tf_op jit(solution)/shard_map/all_to_all | solution.py:19
  182.7 9.5 %all-reduce.1 = (f32[128]{0:T(128)S(1)}, f32[128]{0:T(128)S(1)}) all-reduce(f32[128]{0:T(128)S(1)} %get-tuple-element.107, f32[128]{0:T(128)S(1)} %get-tuple-element.106), channel_id=1, replica_groups=mesh['head_0'=4,'head_1'=4,'batch'=8] {'head_0'}, use_global_device_ids=true, to_apply=%region_11.12 | all-reduce | flops 256 | bytes 2048 | tf_op jit(solution)/shard_map/psum | solution.py:25
  192.2 7.7 %all-reduce = (f32[128]{0:T(128)S(1)}, f32[128]{0:T(128)S(1)}) all-reduce(f32[128]{0:T(128)S(1)} %get-tuple-element.130, f32[128]{0:T(128)S(1)} %get-tuple-element.131), channel_id=1, replica_groups=mesh['head_0'=4,'head_1'=4,'batch'=8] {'head_1'}, use_global_device_ids=true, to_apply=%region_12.13 | all-reduce | flops 256 | bytes 2048 | tf_op jit(solution)/shard_map/psum | solution.py:25
  200.3 16.6 %all_to_all.25 = bf16[16,128,256]{1,2,0:T(8,128)(2,1)} all-to-all(bf16[16,128,256]{1,2,0:T(8,128)(2,1)S(1)} %broadcast_in_dim.21), channel_id=1, replica_groups=mesh['head_0'=4,'head_1'=4,'batch'=8] {'head_0','head_1'}, dimensions={0} | all-to-all | bytes 2097152 | tf_op jit(solution)/shard_map/all_to_all | solution.py:37
  218.4 4.3 %stack.3 = bf16[8,128,4096]{2,1,0:T(8,128)(2,1)} broadcast(bf16[128,4096]{1,0:T(8,128)(2,1)S(1)} %copy.105), dimensions={1,2} | broadcast | bytes 9437184 | tf_op jit(solution)/shard_map/stack | solution.py:220
  222.7 5.1 %all-to-all-start.2 = ((bf16[8,128,4096]{2,1,0:T(8,128)(2,1)}), bf16[8,128,4096]{2,1,0:T(8,128)(2,1)}, u32[]{:S(2)}, u32[]{:S(2)}) async-start(bf16[8,128,4096]{2,1,0:T(8,128)(2,1)} %stack.3), calls=%async_computation.2 | async-start | bytes 16777216 | tf_op jit(solution)/shard_map/all_to_all | solution.py:220
  227.8 100.4 %all-gather = s32[8,16,8]{1,2,0:T(8,128)S(1)} all-gather(s32[1,16,8]{1,2,0:T(8,128)S(1)} %bitcast.137), channel_id=1, replica_groups=mesh['head_0'=4,'head_1'=4,'batch'=8] {'batch'}, dimensions={0}, use_global_device_ids=true | all-gather | bytes 4608 | tf_op jit(solution)/shard_map/all_gather | solution.py:222
  328.5 8.3 %fusion.23 = (f32[1024]{0:T(1024)S(1)}, f32[1024,512]{0,1:T(8,128)S(1)}) fusion(bf16[1024,4096]{1,0:T(8,128)(2,1)} %bitcast.25, bf16[4096,512]{1,0:T(8,128)(2,1)} %param.29), kind=kOutput, calls=%fused_computation.78 | convolution fusion | flops 4295490560 | bytes 14684160 | tf_op jit(solution)/shard_map/dot_general | solution.py:224
  338.0 3.4 all-to-all-start.3
  341.4 6.1 %all-to-all-done.3 = f32[8,3,1024]{2,1,0:T(4,128)S(1)} async-done(((f32[8,3,1024]{2,1,0:T(4,128)}), f32[8,3,1024]{2,1,0:T(4,128)S(1)}, u32[]{:S(2)}, u32[]{:S(2)}) %all-to-all-start.3) | async-done | bytes 98336 | tf_op jit(solution)/shard_map/all_to_all | solution.py:37
  348.7 3.5 all-to-all-start.4
  352.3 7.5 %all-to-all-done.4 = f32[16,3,128]{2,1,0:T(4,128)S(1)} async-done(((f32[16,3,128]{2,1,0:T(4,128)}), f32[16,3,128]{2,1,0:T(4,128)S(1)}, u32[]{:S(2)}, u32[]{:S(2)}) %all-to-all-start.4) | async-done | bytes 24608 | tf_op jit(solution)/shard_map/all_to_all | solution.py:37
  (207 shorter events, 101.7 us)
Async XLA Ops:
  0.6 132.8 %copy-start = (bf16[256,4096]{1,0:T(8,128)(2,1)S(1)}, bf16[256,4096]{1,0:T(8,128)(2,1)}, u32[]{:S(2)}) copy-start(bf16[256,4096]{1,0:T(8,128)(2,1)} %param.27) | copy-start | bytes 6291460
  0.6 5.1 %copy-start.3 = (bf16[128,4096]{1,0:T(8,128)(2,1)S(1)}, bf16[128,4096]{1,0:T(8,128)(2,1)}, u32[]{:S(2)}) copy-start(bf16[128,4096]{1,0:T(8,128)(2,1)} %param.17) | copy-start | bytes 3145732
  7.8 3.8 %copy-start.7 = (f32[256]{0:T(256)S(1)}, f32[256]{0:T(256)}, u32[]{:S(2)}) copy-start(f32[256]{0:T(256)} %param.24) | copy-start | bytes 3076
  22.4 105.5 %copy-start.4 = (f32[16,8,4]{2,1,0:T(8,128)S(1)}, f32[16,8,4]{2,1,0:T(8,128)}, u32[]{:S(2)}) copy-start(f32[16,8,4]{2,1,0:T(8,128)} %get-tuple-element.108) | copy-start | bytes 6148
  22.4 106.1 %copy-start.8 = (f32[256]{0:T(256)S(1)}, f32[256]{0:T(256)}, u32[]{:S(2)}) copy-start(f32[256]{0:T(256)} %param.25) | copy-start | bytes 3076
  22.4 8.2 %copy-start.1 = (f32[16,4,64,64]{3,2,1,0:T(8,128)S(1)}, f32[16,4,64,64]{3,2,1,0:T(8,128)}, u32[]{:S(2)}) copy-start(f32[16,4,64,64]{3,2,1,0:T(8,128)} %get-tuple-element.245) | copy-start | bytes 3145732 | tf_op jit(solution)/shard_map/while
  32.2 3.4 copy-start.2
  35.6 8.2 %copy-start.1 = (f32[16,4,64,64]{3,2,1,0:T(8,128)S(1)}, f32[16,4,64,64]{3,2,1,0:T(8,128)}, u32[]{:S(2)}) copy-start(f32[16,4,64,64]{3,2,1,0:T(8,128)} %get-tuple-element.245) | copy-start | bytes 3145732 | tf_op jit(solution)/shard_map/while
  45.4 3.4 copy-start.2
  48.8 8.2 %copy-start.1 = (f32[16,4,64,64]{3,2,1,0:T(8,128)S(1)}, f32[16,4,64,64]{3,2,1,0:T(8,128)}, u32[]{:S(2)}) copy-start(f32[16,4,64,64]{3,2,1,0:T(8,128)} %get-tuple-element.245) | copy-start | bytes 3145732 | tf_op jit(solution)/shard_map/while
  58.6 3.4 copy-start.2
  62.0 8.2 %copy-start.1 = (f32[16,4,64,64]{3,2,1,0:T(8,128)S(1)}, f32[16,4,64,64]{3,2,1,0:T(8,128)}, u32[]{:S(2)}) copy-start(f32[16,4,64,64]{3,2,1,0:T(8,128)} %get-tuple-element.245) | copy-start | bytes 3145732 | tf_op jit(solution)/shard_map/while
  71.8 3.4 copy-start.2
  75.2 8.2 %copy-start.1 = (f32[16,4,64,64]{3,2,1,0:T(8,128)S(1)}, f32[16,4,64,64]{3,2,1,0:T(8,128)}, u32[]{:S(2)}) copy-start(f32[16,4,64,64]{3,2,1,0:T(8,128)} %get-tuple-element.245) | copy-start | bytes 3145732 | tf_op jit(solution)/shard_map/while
  88.4 8.2 %copy-start.1 = (f32[16,4,64,64]{3,2,1,0:T(8,128)S(1)}, f32[16,4,64,64]{3,2,1,0:T(8,128)}, u32[]{:S(2)}) copy-start(f32[16,4,64,64]{3,2,1,0:T(8,128)} %get-tuple-element.245) | copy-start | bytes 3145732 | tf_op jit(solution)/shard_map/while
  101.5 8.2 %copy-start.1 = (f32[16,4,64,64]{3,2,1,0:T(8,128)S(1)}, f32[16,4,64,64]{3,2,1,0:T(8,128)}, u32[]{:S(2)}) copy-start(f32[16,4,64,64]{3,2,1,0:T(8,128)} %get-tuple-element.245) | copy-start | bytes 3145732 | tf_op jit(solution)/shard_map/while
  114.7 8.2 %copy-start.1 = (f32[16,4,64,64]{3,2,1,0:T(8,128)S(1)}, f32[16,4,64,64]{3,2,1,0:T(8,128)}, u32[]{:S(2)}) copy-start(f32[16,4,64,64]{3,2,1,0:T(8,128)} %get-tuple-element.245) | copy-start | bytes 3145732 | tf_op jit(solution)/shard_map/while
  124.5 3.4 copy-start.2
  140.8 40.1 %all-to-all-start = ((f32[16,128,256]{2,1,0:T(8,128)}), f32[16,128,256]{2,1,0:T(8,128)}, u32[]{:S(2)}, u32[]{:S(2)}) async-start(f32[16,128,256]{2,1,0:T(8,128)} %bitcast.114), calls=%async_computation | async-start | bytes 4194304 | tf_op jit(solution)/shard_map/all_to_all | solution.py:19
  222.7 5.1 %copy-start.5 = (s32[16,8]{0,1:T(8,128)S(1)}, s32[16,8]{0,1:T(8,128)}, u32[]{:S(2)}) copy-start(s32[16,8]{0,1:T(8,128)} %param.30) | copy-start | bytes 1540
  222.7 105.8 %all-to-all-start.2 = ((bf16[8,128,4096]{2,1,0:T(8,128)(2,1)}), bf16[8,128,4096]{2,1,0:T(8,128)(2,1)}, u32[]{:S(2)}, u32[]{:S(2)}) async-start(bf16[8,128,4096]{2,1,0:T(8,128)(2,1)} %stack.3), calls=%async_computation.2 | async-start | bytes 16777216 | tf_op jit(solution)/shard_map/all_to_all | solution.py:220
  336.8 15.4 %copy-start.6 = (s32[16,8]{0,1:T(8,128)S(1)}, s32[16,8]{0,1:T(8,128)}, u32[]{:S(2)}) copy-start(s32[16,8]{0,1:T(8,128)} %param.31) | copy-start | bytes 1540
  338.0 9.5 %all-to-all-start.3 = ((f32[8,3,1024]{2,1,0:T(4,128)}), f32[8,3,1024]{2,1,0:T(4,128)S(1)}, u32[]{:S(2)}, u32[]{:S(2)}) async-start(f32[8,3,1024]{2,1,0:T(4,128)} %broadcast_in_dim.23), calls=%async_computation.3 | async-start | bytes 262144 | tf_op jit(solution)/shard_map/all_to_all | solution.py:37
  348.7 11.0 %all-to-all-start.4 = ((f32[16,3,128]{2,1,0:T(4,128)}), f32[16,3,128]{2,1,0:T(4,128)S(1)}, u32[]{:S(2)}, u32[]{:S(2)}) async-start(f32[16,3,128]{2,1,0:T(4,128)} %broadcast_in_dim.25), calls=%async_computation.4 | async-start | bytes 65536 | tf_op jit(solution)/shard_map/all_to_all | solution.py:37
  (3 other events, 10.1 us)
